TPU v7x, 32 devices: a whole 2x2x4 slice. The times are simulated.
32 devices in a mesh: gx: 4 (over y, core), gy: 2 (over x), gz: 4 (over z).
Axes of the slice: x: 2, y: 2, z: 4, core: 2. Of those that a mesh axis runs over, the one named last changes fastest.
Arguments:
- density: float32 [32, 32, 512], P('gx', 'gy', 'gz'), may hold values from 0.7 to 1.6
- momentum: float32 [32, 32, 512], P('gx', 'gy', 'gz'), may hold values from -7 to 7
- hydrogen: float32 [32, 32, 512], P('gx', 'gy', 'gz'), may hold values from 0.05 to 1.2
- forced_modes: int32 [96, 3], replicated, may hold values from -3 to 3, as said below
Outputs:
- density_rate: float32 [32, 32, 512], P('gx', 'gy', 'gz')
- momentum_rate: float32 [32, 32, 512], P('gx', 'gy', 'gz')
- hydrogen_rate: float32 [32, 32, 512], P('gx', 'gy', 'gz')
Inputs may be any that keep to these rules, and one draw needn't show every extreme that they name: `forced_modes`: each row is a wave vector (kx, ky, kz) with 1 <= kx^2 + ky^2 + kz^2 <= 9; the 96 rows are distinct.
All inputs are finite; a program needn't handle non-finite values.
Results may differ from a plain program's by a relative error of at most 0.0003.
Values sent between devices are 32-bit elements; how exact they have to be, the bound alone decides.
A program may use at most 64 MiB of HBM per device.

v0:
```python
import jax
import jax.numpy as jnp
from jax import lax
from jax.sharding import PartitionSpec as P

KMAX = 3
FIRST_COEFFS = (0.8, -0.2, 4.0 / 105.0, -1.0 / 280.0)
SECOND_COEFFS = (1.6, -0.2, 8.0 / 315.0, -1.0 / 560.0)
CENTRE_COEFF = -205.0 / 72.0
VISCOSITY = 0.3
DIFFUSIVITY = 1.5
FORCE_POWER = 0.3
ENERGY_EPS = 1e-06
ACTIVATION = 2.0
HIGHEST = lax.Precision.HIGHEST


def padded_2(x, sides, width):
    for axis, dim in sides:
        size, length = (lax.axis_size(axis), x.shape[dim])
        up = [(i, (i + 1) % size) for i in range(size)]
        down = [(j, i) for i, j in up]
        last = lax.slice_in_dim(x, length - width, length, axis=dim)
        first = lax.slice_in_dim(x, 0, width, axis=dim)
        before = lax.ppermute(last, axis, up)
        after = lax.ppermute(first, axis, down)
        x = jnp.concatenate([before, x, after], axis=dim)
    return x


def shifted(padded, axis, offset, length):
    return lax.slice_in_dim(padded, 4 + offset, 4 + offset + length, axis=axis)


def first_diff(padded, axis, length):
    total = jnp.zeros_like(shifted(padded, axis, 0, length))
    for offset, weight in enumerate(FIRST_COEFFS, 1):
        total = total + weight * (
            shifted(padded, axis, offset, length) - shifted(padded, axis, -offset, length)
        )
    return total


def second_diff(padded, axis, length):
    total = CENTRE_COEFF * shifted(padded, axis, 0, length)
    for offset, weight in enumerate(SECOND_COEFFS, 1):
        total = total + weight * (
            shifted(padded, axis, offset, length) + shifted(padded, axis, -offset, length)
        )
    return total


def wave_tables(start, local, total):
    position = start + jnp.arange(local, dtype=jnp.int32)
    wavenum = jnp.arange(-KMAX, KMAX + 1, dtype=jnp.int32)
    phase = wavenum[:, None] * position[None, :] % total
    angle = 2.0 * jnp.pi / total * phase.astype(jnp.float32)
    return (jnp.cos(angle), jnp.sin(angle))


def modal_force(velocity, forced_modes):
    size_x, size_y, size_z = velocity.shape
    full_x = size_x * lax.axis_size("gx")
    full_y = size_y * lax.axis_size("gy")
    full_z = size_z * lax.axis_size("gz")
    cos_x, sin_x = wave_tables(lax.axis_index("gx") * size_x, size_x, full_x)
    cos_y, sin_y = wave_tables(lax.axis_index("gy") * size_y, size_y, full_y)
    cos_z, sin_z = wave_tables(lax.axis_index("gz") * size_z, size_z, full_z)
    flat = velocity.reshape(size_x * size_y, size_z)
    contract = (((1,), (1,)), ((), ()))
    part_re = lax.dot_general(cos_z, flat, contract, precision=HIGHEST).reshape(-1, size_x, size_y)
    part_im = lax.dot_general(sin_z, flat, contract, precision=HIGHEST).reshape(-1, size_x, size_y)
    mid_re = jnp.einsum("axy,by->abx", part_re, cos_y, precision=HIGHEST) - jnp.einsum(
        "axy,by->abx", part_im, sin_y, precision=HIGHEST
    )
    mid_im = jnp.einsum("axy,by->abx", part_re, sin_y, precision=HIGHEST) + jnp.einsum(
        "axy,by->abx", part_im, cos_y, precision=HIGHEST
    )
    cube_re = jnp.einsum("abx,cx->cba", mid_re, cos_x, precision=HIGHEST) - jnp.einsum(
        "abx,cx->cba", mid_im, sin_x, precision=HIGHEST
    )
    cube_im = jnp.einsum("abx,cx->cba", mid_re, sin_x, precision=HIGHEST) + jnp.einsum(
        "abx,cx->cba", mid_im, cos_x, precision=HIGHEST
    )
    width = 2 * KMAX + 1
    code = (
        (forced_modes[:, 0] + KMAX) * width * width
        + (forced_modes[:, 1] + KMAX) * width
        + (forced_modes[:, 2] + KMAX)
    )
    selector = (code[:, None] == jnp.arange(width**3, dtype=jnp.int32)[None, :]).astype(jnp.float32)
    local_cos = jnp.dot(selector, cube_re.reshape(-1), precision=HIGHEST)
    local_sin = jnp.dot(selector, cube_im.reshape(-1), precision=HIGHEST)
    summed = lax.psum((local_cos, local_sin), ("gx", "gy", "gz"))
    ncell = float(full_x * full_y * full_z)
    coef_cos = summed[0] / ncell
    coef_sin = summed[1] / ncell
    energy = jnp.sum(coef_cos * coef_cos + coef_sin * coef_sin)
    spec_re = jnp.dot(selector.T, coef_cos, precision=HIGHEST).reshape(width, width, width)
    spec_im = -jnp.dot(selector.T, coef_sin, precision=HIGHEST).reshape(width, width, width)
    step_re = jnp.einsum("abc,ax->xbc", spec_re, cos_x, precision=HIGHEST) - jnp.einsum(
        "abc,ax->xbc", spec_im, sin_x, precision=HIGHEST
    )
    step_im = jnp.einsum("abc,ax->xbc", spec_re, sin_x, precision=HIGHEST) + jnp.einsum(
        "abc,ax->xbc", spec_im, cos_x, precision=HIGHEST
    )
    plane_re = jnp.einsum("xbc,by->xyc", step_re, cos_y, precision=HIGHEST) - jnp.einsum(
        "xbc,by->xyc", step_im, sin_y, precision=HIGHEST
    )
    plane_im = jnp.einsum("xbc,by->xyc", step_re, sin_y, precision=HIGHEST) + jnp.einsum(
        "xbc,by->xyc", step_im, cos_y, precision=HIGHEST
    )
    low = 2.0 * (
        jnp.dot(plane_re.reshape(-1, width), cos_z, precision=HIGHEST)
        - jnp.dot(plane_im.reshape(-1, width), sin_z, precision=HIGHEST)
    )
    return FORCE_POWER * low.reshape(size_x, size_y, size_z) / (energy + ENERGY_EPS)


def stencil_terms(density, momentum, hydrogen):
    size_x, size_y, size_z = density.shape
    fields = jnp.stack([density, momentum, hydrogen])
    stream_pad = padded_2(fields, (("gx", 1),), 4)
    dens_pad = stream_pad[0]
    mom_pad = stream_pad[1]
    fuel_pad = stream_pad[2]
    vel_pad = mom_pad / dens_pad
    velocity = momentum / density
    mass_div = first_diff(mom_pad, 0, size_x)
    mom_div = first_diff(mom_pad * vel_pad + dens_pad, 0, size_x)
    fuel_div = first_diff(fuel_pad * vel_pad, 0, size_x)
    diffused = second_diff(stream_pad[1:], 1, size_x)
    carried = fields[1:]
    side_pad = padded_2(carried, (("gy", 2),), 4)
    diffused = diffused + second_diff(side_pad, 2, size_y)
    depth_pad = padded_2(carried, (("gz", 3),), 4)
    diffused = diffused + second_diff(depth_pad, 3, size_z)
    density_rate = -mass_div
    momentum_part = -mom_div + VISCOSITY * diffused[0]
    hydrogen_rate = (
        -fuel_div + DIFFUSIVITY * diffused[1] - hydrogen * jnp.exp(-ACTIVATION * hydrogen / density)
    )
    return (density_rate, momentum_part, hydrogen_rate, velocity)


def per_device(density, momentum, hydrogen, forced_modes):
    density_rate, momentum_part, hydrogen_rate, velocity = stencil_terms(
        density, momentum, hydrogen
    )
    force = modal_force(velocity, forced_modes)
    momentum_rate = momentum_part + density * force
    return (density_rate, momentum_rate, hydrogen_rate)


def solution(mesh):
    in_specs = (P("gx", "gy", "gz"), P("gx", "gy", "gz"), P("gx", "gy", "gz"), P())
    out_specs = (P("gx", "gy", "gz"), P("gx", "gy", "gz"), P("gx", "gy", "gz"))
    return jax.shard_map(
        per_device, mesh=mesh, in_specs=in_specs, out_specs=out_specs, check_vma=False
    )
```

profile of v0, /device:TPU:0, one launch (start us, length us, event | category | flops | bytes accessed | tf_op | source)
XLA Modules:
  0.0 68.3 jit_solution(13561486433452275139)
XLA Ops:
  0.6 0.9 %pad_maximum_fusion.4 = f32[3,8,16,128]{3,2,1,0:T(8,128)S(1)} fusion(f32[1,8,16,128]{3,2,1,0:T(8,128)} %bitcast.128, f32[1,8,16,128]{3,2,1,0:T(8,128)} %bitcast.136, f32[1,8,16,128]{3,2,1,0:T(8,128)} %bitcast.144), kind=kLoop, calls=%fused_computation.35 | loop fusion | flops 98304 | bytes 393216 | tf_op jit(solution)/shard_map/stack | solution.py:122
  1.6 2.5 %collective-permute-start = (f32[3,4,16,128]{3,2,1,0:T(8,128)S(1)}, f32[3,4,16,128]{3,2,1,0:T(8,128)S(1)}, u32[]{:S(2)}, u32[]{:S(2)}) collective-permute-start(f32[3,4,16,128]{3,2,1,0:T(8,128)S(1)} %get-tuple-element.9), channel_id=1, source_target_pairs={{8,0},{16,8},{24,16},{0,24},{9,1},{17,9},{25,17},{1,25},{10,2},{18... | collective-permute-start | bytes 294920 | tf_op jit(solution)/shard_map/ppermute | solution.py:26
  4.2 3.7 %collective-permute-start.4 = (f32[2,8,16,4]{3,2,1,0:T(8,128)S(1)}, f32[2,8,16,4]{3,2,1,0:T(8,128)S(1)}, u32[]{:S(2)}, u32[]{:S(2)}) collective-permute-start(f32[2,8,16,4]{3,2,1,0:T(8,128)S(1)} %get-tuple-element.17), channel_id=1, source_target_pairs={{1,0},{2,1},{3,2},{0,3},{5,4},{6,5},{7,6},{4,7},{9,8},{10,9},{11,1... | collective-permute-start | bytes 12296 | tf_op jit(solution)/shard_map/ppermute | solution.py:26
  7.9 1.6 %collective-permute-start.2 = (f32[2,8,4,128]{3,2,1,0:T(4,128)S(1)}, f32[2,8,4,128]{3,2,1,0:T(4,128)S(1)}, u32[]{:S(2)}, u32[]{:S(2)}) collective-permute-start(f32[2,8,4,128]{3,2,1,0:T(4,128)S(1)} %get-tuple-element.13), channel_id=1, source_target_pairs={{4,0},{0,4},{5,1},{1,5},{6,2},{2,6},{7,3},{3,7},{12,8},{8,12},{13,... | collective-permute-start | bytes 98312 | tf_op jit(solution)/shard_map/ppermute | solution.py:26
  9.4 0.6 fusion.109
  10.1 0.7 fusion.102
  10.7 0.5 fusion.86
  11.3 0.5 fusion.84
  11.8 0.5 fusion.7
  12.3 0.6 fusion.97
  12.9 0.6 fusion.112
  13.5 0.6 fusion.6
  14.1 0.6 fusion.4
  15.0 0.6 copy-done.3
  15.5 0.6 fusion.5
  16.9 39.2 %all-reduce = (f32[96]{0:T(128)S(1)}, f32[96]{0:T(128)S(1)}) all-reduce(f32[96]{0:T(128)S(1)} %convolution_bitcast_fusion.1, f32[96]{0:T(128)S(1)} %convolution_bitcast_fusion), channel_id=1, replica_groups=mesh['gx'=4,'gy'=2,'gz'=4] {'gx','gy','gz'}, use_global_device_ids=true, to_apply=%region_0.1 | all-reduce | flops 192 | bytes 1536 | tf_op jit(solution)/shard_map/psum | solution.py:94
  56.4 0.3 fusion.80
  56.7 0.3 fusion.78
  57.3 0.3 convolution_subtract_fusion.2
  57.8 0.3 fusion.117
  58.1 0.3 fusion.104
  58.4 0.6 add_reduce_fusion
  59.4 0.3 fusion.3
  59.8 0.3 fusion.123
  60.1 0.3 fusion.2
  61.1 0.3 fusion.1
  61.5 2.3 %collective-permute-start.3 = (f32[2,8,4,128]{3,2,1,0:T(4,128)S(1)}, f32[2,8,4,128]{3,2,1,0:T(4,128)S(1)}, u32[]{:S(2)}, u32[]{:S(2)}) collective-permute-start(f32[2,8,4,128]{3,2,1,0:T(4,128)S(1)} %get-tuple-element.14), channel_id=1, source_target_pairs={{0,4},{4,0},{1,5},{5,1},{2,6},{6,2},{3,7},{7,3},{8,12},{12,8},{9,1... | collective-permute-start | bytes 98312 | tf_op jit(solution)/shard_map/ppermute | solution.py:25
  64.0 1.7 %collective-permute-done.3 = f32[2,8,4,128]{3,2,1,0:T(4,128)S(1)} collective-permute-done((f32[2,8,4,128]{3,2,1,0:T(4,128)S(1)}, f32[2,8,4,128]{3,2,1,0:T(4,128)S(1)}, u32[]{:S(2)}, u32[]{:S(2)}) %collective-permute-start.3) | collective-permute-done | bytes 32800 | tf_op jit(solution)/shard_map/ppermute | solution.py:25
  65.9 0.7 fusion.68
  66.6 0.3 fusion.14
  66.9 0.7 %fusion.45 = f32[8,16,128]{2,1,0:T(8,128)} fusion(f32[2,8,16,128]{3,2,1,0:T(8,128)S(1)} %fusion.14, f32[16,16,128]{2,1,0:T(8,128)S(1)} %get-tuple-element.5, f32[8,16,128]{2,1,0:T(8,128)S(1)} %copy-done, f32[8,16,128]{2,1,0:T(8,128)S(1)} %copy-done.2), kind=kLoop, calls=%fused_computation.94 | loop fusion | flops 294912 | bytes 786432 | tf_op jit(solution)/shard_map/sub | solution.py:141
  67.6 0.7 fusion.56
  (43 shorter events, 2.9 us)
Async XLA Ops:
  1.6 2.5 %copy-start = (f32[8,16,128]{2,1,0:T(8,128)S(1)}, f32[8,16,128]{2,1,0:T(8,128)}, u32[]{:S(2)}) copy-start(f32[8,16,128]{2,1,0:T(8,128)} %param.6) | copy-start | bytes 196612
  1.6 2.5 %copy-start.1 = (f32[8,16,128]{2,1,0:T(8,128)S(1)}, f32[8,16,128]{2,1,0:T(8,128)}, u32[]{:S(2)}) copy-start(f32[8,16,128]{2,1,0:T(8,128)} %param.5) | copy-start | bytes 196612
  1.6 64.2 %collective-permute-start = (f32[3,4,16,128]{3,2,1,0:T(8,128)S(1)}, f32[3,4,16,128]{3,2,1,0:T(8,128)S(1)}, u32[]{:S(2)}, u32[]{:S(2)}) collective-permute-start(f32[3,4,16,128]{3,2,1,0:T(8,128)S(1)} %get-tuple-element.9), channel_id=1, source_target_pairs={{8,0},{16,8},{24,16},{0,24},{9,1},{17,9},{25,17},{1,25},{10,2},{18... | collective-permute-start | bytes 294920 | tf_op jit(solution)/shard_map/ppermute | solution.py:26
  4.1 61.7 %collective-permute-start.1 = (f32[3,4,16,128]{3,2,1,0:T(8,128)S(1)}, f32[3,4,16,128]{3,2,1,0:T(8,128)S(1)}, u32[]{:S(2)}, u32[]{:S(2)}) collective-permute-start(f32[3,4,16,128]{3,2,1,0:T(8,128)S(1)} %get-tuple-element.10), channel_id=1, source_target_pairs={{0,8},{8,16},{16,24},{24,0},{1,9},{9,17},{17,25},{25,1},{2,10},{10... | collective-permute-start | bytes 294920 | tf_op jit(solution)/shard_map/ppermute | solution.py:25
  4.2 57.3 %collective-permute-start.4 = (f32[2,8,16,4]{3,2,1,0:T(8,128)S(1)}, f32[2,8,16,4]{3,2,1,0:T(8,128)S(1)}, u32[]{:S(2)}, u32[]{:S(2)}) collective-permute-start(f32[2,8,16,4]{3,2,1,0:T(8,128)S(1)} %get-tuple-element.17), channel_id=1, source_target_pairs={{1,0},{2,1},{3,2},{0,3},{5,4},{6,5},{7,6},{4,7},{9,8},{10,9},{11,1... | collective-permute-start | bytes 12296 | tf_op jit(solution)/shard_map/ppermute | solution.py:26
  7.9 1.6 %copy-start.2 = (f32[8,16,128]{2,1,0:T(8,128)S(1)}, f32[8,16,128]{2,1,0:T(8,128)}, u32[]{:S(2)}) copy-start(f32[8,16,128]{2,1,0:T(8,128)} %param.4) | copy-start | bytes 196612
  7.9 56.0 %collective-permute-start.5 = (f32[2,8,16,4]{3,2,1,0:T(8,128)S(1)}, f32[2,8,16,4]{3,2,1,0:T(8,128)S(1)}, u32[]{:S(2)}, u32[]{:S(2)}) collective-permute-start(f32[2,8,16,4]{3,2,1,0:T(8,128)S(1)} %get-tuple-element.18), channel_id=1, source_target_pairs={{0,1},{1,2},{2,3},{3,0},{4,5},{5,6},{6,7},{7,4},{8,9},{9,10},{10,1... | collective-permute-start | bytes 12296 | tf_op jit(solution)/shard_map/ppermute | solution.py:25
  7.9 56.1 %collective-permute-start.2 = (f32[2,8,4,128]{3,2,1,0:T(4,128)S(1)}, f32[2,8,4,128]{3,2,1,0:T(4,128)S(1)}, u32[]{:S(2)}, u32[]{:S(2)}) collective-permute-start(f32[2,8,4,128]{3,2,1,0:T(4,128)S(1)} %get-tuple-element.13), channel_id=1, source_target_pairs={{4,0},{0,4},{5,1},{1,5},{6,2},{2,6},{7,3},{3,7},{12,8},{8,12},{13,... | collective-permute-start | bytes 98312 | tf_op jit(solution)/shard_map/ppermute | solution.py:26
  14.8 0.7 %copy-start.3 = (s32[96,3]{0,1:T(4,128)S(1)}, s32[96,3]{0,1:T(4,128)}, u32[]{:S(2)}) copy-start(s32[96,3]{0,1:T(4,128)} %param.7) | copy-start | bytes 3460
  61.5 4.2 %collective-permute-start.3 = (f32[2,8,4,128]{3,2,1,0:T(4,128)S(1)}, f32[2,8,4,128]{3,2,1,0:T(4,128)S(1)}, u32[]{:S(2)}, u32[]{:S(2)}) collective-permute-start(f32[2,8,4,128]{3,2,1,0:T(4,128)S(1)} %get-tuple-element.14), channel_id=1, source_target_pairs={{0,4},{4,0},{1,5},{5,1},{2,6},{6,2},{3,7},{7,3},{8,12},{12,8},{9,1... | collective-permute-start | bytes 98312 | tf_op jit(solution)/shard_map/ppermute | solution.py:25
where the time goes:
time: 68.6 us; the launch traced here: 68.3 us
  blocking collectives  39.2 us (57%)
  starting transfers between devices  10.1 us (15%)
  matrix products  9.66 us (14%)
  other arithmetic  4.3 us (6%)
  local copies, waits for them, and re-layouts  1.83 us (3%)
  waiting for transfers between devices  1.76 us (3%)
  between operations  1.52 us (2%)
    psum x1, blocking collectives, modal_force(): summed = lax.psum((local_cos, local_sin), ('gx', 'gy', 'gz'))  39.2 us
    ppermute x3, starting transfers between devices, padded_2(): after = lax.ppermute(first, axis, down)  7.7 us
    ppermute x3, starting transfers between devices, padded_2(): before = lax.ppermute(last, axis, up)  2.35 us
    ppermute x3, waiting for transfers between devices, padded_2(): before = lax.ppermute(last, axis, up)  1.75 us
  transfers between devices with their start and end apart: 6, of which 1 were waited for; matrix products, arithmetic and copies ran while one was open for 17% of the time, Pallas kernels for 0%

commit v1 on v0

--- a/solution.py
+++ b/solution.py
@@ -13,6 +13,10 @@
 ENERGY_EPS = 1e-06
 ACTIVATION = 2.0
 HIGHEST = lax.Precision.HIGHEST
+
+
+def lines_apply(w_in, which_axis, net_axis):
+    return lax.psum(lax.psum(w_in, which_axis), net_axis)
 
 
 def padded_2(x, sides, width):
@@ -91,7 +95,7 @@
     selector = (code[:, None] == jnp.arange(width**3, dtype=jnp.int32)[None, :]).astype(jnp.float32)
     local_cos = jnp.dot(selector, cube_re.reshape(-1), precision=HIGHEST)
     local_sin = jnp.dot(selector, cube_im.reshape(-1), precision=HIGHEST)
-    summed = lax.psum((local_cos, local_sin), ("gx", "gy", "gz"))
+    summed = lines_apply((local_cos, local_sin), "gx", ("gy", "gz"))
     ncell = float(full_x * full_y * full_z)
     coef_cos = summed[0] / ncell
     coef_sin = summed[1] / ncell

time: 68.6 us -> 56.9 us (0.83)
  blocking collectives: 39.2 us -> 27.7 us
  starting transfers between devices: 10.1 us -> 9.26 us
    psum x1 -> x2, blocking collectives: 39.2 us -> 27.7 us  [lines_apply(): return lax.psum(lax.psum(w_in, which_axis), net_axis)]
    ppermute x3, starting transfers between devices: 2.35 us -> 1.56 us  [padded_2(): before = lax.ppermute(last, axis, up)]
  transfers between devices with their start and end apart: 6 -> 6, of which waited for: 1 -> 1; matrix products, arithmetic and copies ran while one was open for 17% -> 21% of each run, Pallas kernels for 0% -> 0%
where the time goes in v1:
time: 56.9 us; the launch traced here: 56.6 us
  blocking collectives  27.7 us (49%)
  matrix products  9.67 us (17%)
  starting transfers between devices  9.26 us (16%)
  other arithmetic  4.3 us (8%)
  waiting for transfers between devices  2.29 us (4%)
  local copies, waits for them, and re-layouts  1.82 us (3%)
  between operations  1.53 us (3%)
    psum x2, blocking collectives, lines_apply(): return lax.psum(lax.psum(w_in, which_axis), net_axis)  27.7 us
    ppermute x3, starting transfers between devices, padded_2(): after = lax.ppermute(first, axis, down)  7.7 us
    ppermute x3, waiting for transfers between devices, padded_2(): before = lax.ppermute(last, axis, up)  2.28 us
    ppermute x3, starting transfers between devices, padded_2(): before = lax.ppermute(last, axis, up)  1.56 us
  transfers between devices with their start and end apart: 6, of which 1 were waited for; matrix products, arithmetic and copies ran while one was open for 21% of the time, Pallas kernels for 0%

profile of v1, /device:TPU:0, one launch (start us, length us, event | category | flops | bytes accessed | tf_op | source)
XLA Modules:
  0.0 56.6 jit_solution(10331776919333260888)
XLA Ops:
  0.6 0.9 %pad_maximum_fusion.4 = f32[3,8,16,128]{3,2,1,0:T(8,128)S(1)} fusion(f32[1,8,16,128]{3,2,1,0:T(8,128)} %bitcast.128, f32[1,8,16,128]{3,2,1,0:T(8,128)} %bitcast.136, f32[1,8,16,128]{3,2,1,0:T(8,128)} %bitcast.144), kind=kLoop, calls=%fused_computation.35 | loop fusion | flops 98304 | bytes 393216 | tf_op jit(solution)/shard_map/stack | solution.py:126
  1.6 2.5 %collective-permute-start = (f32[3,4,16,128]{3,2,1,0:T(8,128)S(1)}, f32[3,4,16,128]{3,2,1,0:T(8,128)S(1)}, u32[]{:S(2)}, u32[]{:S(2)}) collective-permute-start(f32[3,4,16,128]{3,2,1,0:T(8,128)S(1)} %get-tuple-element.11), channel_id=1, source_target_pairs={{8,0},{16,8},{24,16},{0,24},{9,1},{17,9},{25,17},{1,25},{10,2},{18... | collective-permute-start | bytes 294920 | tf_op jit(solution)/shard_map/ppermute | solution.py:30
  4.2 3.7 %collective-permute-start.4 = (f32[2,8,16,4]{3,2,1,0:T(8,128)S(1)}, f32[2,8,16,4]{3,2,1,0:T(8,128)S(1)}, u32[]{:S(2)}, u32[]{:S(2)}) collective-permute-start(f32[2,8,16,4]{3,2,1,0:T(8,128)S(1)} %get-tuple-element.19), channel_id=1, source_target_pairs={{1,0},{2,1},{3,2},{0,3},{5,4},{6,5},{7,6},{4,7},{9,8},{10,9},{11,1... | collective-permute-start | bytes 12296 | tf_op jit(solution)/shard_map/ppermute | solution.py:30
  7.9 1.6 %collective-permute-start.2 = (f32[2,8,4,128]{3,2,1,0:T(4,128)S(1)}, f32[2,8,4,128]{3,2,1,0:T(4,128)S(1)}, u32[]{:S(2)}, u32[]{:S(2)}) collective-permute-start(f32[2,8,4,128]{3,2,1,0:T(4,128)S(1)} %get-tuple-element.15), channel_id=1, source_target_pairs={{4,0},{0,4},{5,1},{1,5},{6,2},{2,6},{7,3},{3,7},{12,8},{8,12},{13,... | collective-permute-start | bytes 98312 | tf_op jit(solution)/shard_map/ppermute | solution.py:30
  9.4 0.6 %fusion.109 = f32[7,8,16]{2,0,1:T(8,128)S(1)} fusion(s32[128]{0:T(128)S(1)} %iota_add_fusion, s32[7]{0:T(128)S(1)} %iota_add_fusion.3, f32[8,16,128]{2,1,0:T(8,128)S(1)} %copy-done.1, f32[8,16,128]{2,1,0:T(8,128)S(1)} %copy-done.2), kind=kOutput, calls=%fused_computation.186 | convolution fusion | flops 1405184 | bytes 135196 | tf_op jit(solution)/shard_map/dot_general | solution.py:75
  10.1 0.7 %fusion.102 = f32[7,8,16]{2,0,1:T(8,128)S(1)} fusion(s32[128]{0:T(128)S(1)} %iota_add_fusion, s32[7]{0:T(128)S(1)} %iota_add_fusion.3, f32[8,16,128]{2,1,0:T(8,128)S(1)} %copy-done.1, f32[8,16,128]{2,1,0:T(8,128)S(1)} %copy-done.2), kind=kOutput, calls=%fused_computation.179 | convolution fusion | flops 1405184 | bytes 135196 | tf_op jit(solution)/shard_map/dot_general | solution.py:76
  10.7 0.5 fusion.86
  11.3 0.5 fusion.84
  11.8 0.5 fusion.7
  12.3 0.6 %fusion.97 = f32[7,7,7]{2,0,1:T(8,128)S(1)} fusion(f32[7,7,8]{2,1,0:T(8,128)S(1)} %fusion.7, s32[8]{0:T(128)S(1)} %iota_add_fusion.1, s32[7]{0:T(128)S(1)} %iota_add_fusion.3), kind=kOutput, calls=%fused_computation.174 | convolution fusion | flops 33712 | bytes 3000 | tf_op jit(solution)/shard_map/abx,cx->cba/dot_general | solution.py:86
  12.9 0.6 %fusion.112 = f32[7,7,7]{2,0,1:T(8,128)S(1)} fusion(f32[7,7,8]{2,1,0:T(8,128)S(1)} %fusion.7, s32[8]{0:T(128)S(1)} %iota_add_fusion.1, s32[7]{0:T(128)S(1)} %iota_add_fusion.3), kind=kOutput, calls=%fused_computation.189 | convolution fusion | flops 33712 | bytes 3000 | tf_op jit(solution)/shard_map/abx,cx->cba/dot_general | solution.py:83
  13.5 0.6 fusion.6
  14.1 0.6 %fusion.4 = f32[7,7,7]{1,0,2:T(8,128)S(1)} fusion(f32[7,7,7]{2,0,1:T(8,128)S(1)} %fusion.97, f32[7,7,8]{2,1,0:T(8,128)S(1)} %fusion.6, s32[8]{0:T(128)S(1)} %iota_add_fusion.1, s32[7]{0:T(128)S(1)} %iota_add_fusion.3), kind=kOutput, calls=%fused_computation.10 | convolution fusion | flops 34055 | bytes 4372 | tf_op jit(solution)/shard_map/abx,cx->cba/dot_general | solution.py:86
  15.0 0.6 copy-done.3
  15.5 0.6 %fusion.5 = f32[7,7,7]{1,0,2:T(8,128)S(1)} fusion(f32[7,7,7]{2,0,1:T(8,128)S(1)} %fusion.112, f32[7,7,8]{2,1,0:T(8,128)S(1)} %fusion.6, s32[8]{0:T(128)S(1)} %iota_add_fusion.1, s32[7]{0:T(128)S(1)} %iota_add_fusion.3), kind=kOutput, calls=%fused_computation.12 | convolution fusion | flops 34055 | bytes 4372 | tf_op jit(solution)/shard_map/abx,cx->cba/dot_general | solution.py:83
  16.9 6.9 %all-reduce.1 = (f32[96]{0:T(128)S(1)}, f32[96]{0:T(128)S(1)}) all-reduce(f32[96]{0:T(128)S(1)} %convolution_bitcast_fusion.1, f32[96]{0:T(128)S(1)} %convolution_bitcast_fusion), channel_id=1, replica_groups=mesh['gx'=4,'gy'=2,'gz'=4] {'gx'}, use_global_device_ids=true, to_apply=%region_0.1 | all-reduce | flops 192 | bytes 1536 | tf_op jit(solution)/shard_map/psum | solution.py:19
  23.8 20.8 %all-reduce = (f32[96]{0:T(128)S(1)}, f32[96]{0:T(128)S(1)}) all-reduce(f32[96]{0:T(128)S(1)} %get-tuple-element.5, f32[96]{0:T(128)S(1)} %get-tuple-element.6), channel_id=1, replica_groups=mesh['gx'=4,'gy'=2,'gz'=4] {'gy','gz'}, use_global_device_ids=true, to_apply=%region_1.2 | all-reduce | flops 192 | bytes 1536 | tf_op jit(solution)/shard_map/psum | solution.py:19
  45.2 0.3 fusion.78
  45.9 0.3 convolution_subtract_fusion.2
  46.3 0.3 fusion.104
  46.6 0.3 fusion.117
  46.9 0.6 %add_reduce_fusion = f32[]{:T(128)} fusion(f32[96]{0:T(128)S(1)} %get-tuple-element.4, f32[96]{0:T(128)S(1)} %get-tuple-element.3), kind=kLoop, calls=%fused_computation.207 | loop fusion | flops 575 | bytes 772 | tf_op jit(solution)/shard_map/reduce_sum | solution.py:102
  48.0 0.3 fusion.2
  48.3 0.3 fusion.3
  48.7 0.3 fusion.123
  49.7 0.3 fusion.1
  50.0 1.6 %collective-permute-start.3 = (f32[2,8,4,128]{3,2,1,0:T(4,128)S(1)}, f32[2,8,4,128]{3,2,1,0:T(4,128)S(1)}, u32[]{:S(2)}, u32[]{:S(2)}) collective-permute-start(f32[2,8,4,128]{3,2,1,0:T(4,128)S(1)} %get-tuple-element.16), channel_id=1, source_target_pairs={{0,4},{4,0},{1,5},{5,1},{2,6},{6,2},{3,7},{7,3},{8,12},{12,8},{9,1... | collective-permute-start | bytes 98312 | tf_op jit(solution)/shard_map/ppermute | solution.py:29
  51.8 2.3 %collective-permute-done.3 = f32[2,8,4,128]{3,2,1,0:T(4,128)S(1)} collective-permute-done((f32[2,8,4,128]{3,2,1,0:T(4,128)S(1)}, f32[2,8,4,128]{3,2,1,0:T(4,128)S(1)}, u32[]{:S(2)}, u32[]{:S(2)}) %collective-permute-start.3) | collective-permute-done | bytes 32800 | tf_op jit(solution)/shard_map/ppermute | solution.py:29
  54.2 0.7 %fusion.68 = f32[8,16,128]{2,1,0:T(8,128)} fusion(f32[3,12,16,128]{3,2,1,0:T(8,128)S(1)} %get-tuple-element.10, f32[3,12,16,128]{3,2,1,0:T(8,128)S(1)} %get-tuple-element.9), kind=kLoop, calls=%fused_computation.127 | loop fusion | flops 196608 | bytes 589824 | tf_op jit(solution)/shard_map/neg | solution.py:142
  54.9 0.3 fusion.14
  55.2 0.7 %fusion.45 = f32[8,16,128]{2,1,0:T(8,128)} fusion(f32[2,8,16,128]{3,2,1,0:T(8,128)S(1)} %fusion.14, f32[16,16,128]{2,1,0:T(8,128)S(1)} %get-tuple-element.7, f32[8,16,128]{2,1,0:T(8,128)S(1)} %copy-done, f32[8,16,128]{2,1,0:T(8,128)S(1)} %copy-done.2), kind=kLoop, calls=%fused_computation.94 | loop fusion | flops 294912 | bytes 786432 | tf_op jit(solution)/shard_map/sub | solution.py:145
  55.9 0.7 %fusion.56 = f32[8,16,128]{2,1,0:T(8,128)} fusion(f32[2,8,16,128]{3,2,1,0:T(8,128)S(1)} %fusion.14, f32[16,16,128]{2,1,0:T(8,128)S(1)} %get-tuple-element.8, f32[8,16,128]{2,1,0:T(8,128)S(1)} %copy-done.2, f32[8,16,128]{2,1,0:T(8,128)S(1)} %bitcast.147), kind=kLoop, calls=%fused_computation.110 | loop fusion | flops 262144 | bytes 786432 | tf_op jit(solution)/shard_map/add | solution.py:155
  (44 shorter events, 3.2 us)
Async XLA Ops:
  1.6 2.5 %copy-start = (f32[8,16,128]{2,1,0:T(8,128)S(1)}, f32[8,16,128]{2,1,0:T(8,128)}, u32[]{:S(2)}) copy-start(f32[8,16,128]{2,1,0:T(8,128)} %param.6) | copy-start | bytes 196612
  1.6 2.5 %copy-start.1 = (f32[8,16,128]{2,1,0:T(8,128)S(1)}, f32[8,16,128]{2,1,0:T(8,128)}, u32[]{:S(2)}) copy-start(f32[8,16,128]{2,1,0:T(8,128)} %param.5) | copy-start | bytes 196612
  1.6 52.5 %collective-permute-start = (f32[3,4,16,128]{3,2,1,0:T(8,128)S(1)}, f32[3,4,16,128]{3,2,1,0:T(8,128)S(1)}, u32[]{:S(2)}, u32[]{:S(2)}) collective-permute-start(f32[3,4,16,128]{3,2,1,0:T(8,128)S(1)} %get-tuple-element.11), channel_id=1, source_target_pairs={{8,0},{16,8},{24,16},{0,24},{9,1},{17,9},{25,17},{1,25},{10,2},{18... | collective-permute-start | bytes 294920 | tf_op jit(solution)/shard_map/ppermute | solution.py:30
  4.1 50.0 %collective-permute-start.1 = (f32[3,4,16,128]{3,2,1,0:T(8,128)S(1)}, f32[3,4,16,128]{3,2,1,0:T(8,128)S(1)}, u32[]{:S(2)}, u32[]{:S(2)}) collective-permute-start(f32[3,4,16,128]{3,2,1,0:T(8,128)S(1)} %get-tuple-element.12), channel_id=1, source_target_pairs={{0,8},{8,16},{16,24},{24,0},{1,9},{9,17},{17,25},{25,1},{2,10},{10... | collective-permute-start | bytes 294920 | tf_op jit(solution)/shard_map/ppermute | solution.py:29
  4.2 45.8 %collective-permute-start.4 = (f32[2,8,16,4]{3,2,1,0:T(8,128)S(1)}, f32[2,8,16,4]{3,2,1,0:T(8,128)S(1)}, u32[]{:S(2)}, u32[]{:S(2)}) collective-permute-start(f32[2,8,16,4]{3,2,1,0:T(8,128)S(1)} %get-tuple-element.19), channel_id=1, source_target_pairs={{1,0},{2,1},{3,2},{0,3},{5,4},{6,5},{7,6},{4,7},{9,8},{10,9},{11,1... | collective-permute-start | bytes 12296 | tf_op jit(solution)/shard_map/ppermute | solution.py:30
  7.9 1.6 %copy-start.2 = (f32[8,16,128]{2,1,0:T(8,128)S(1)}, f32[8,16,128]{2,1,0:T(8,128)}, u32[]{:S(2)}) copy-start(f32[8,16,128]{2,1,0:T(8,128)} %param.4) | copy-start | bytes 196612
  7.9 43.8 %collective-permute-start.5 = (f32[2,8,16,4]{3,2,1,0:T(8,128)S(1)}, f32[2,8,16,4]{3,2,1,0:T(8,128)S(1)}, u32[]{:S(2)}, u32[]{:S(2)}) collective-permute-start(f32[2,8,16,4]{3,2,1,0:T(8,128)S(1)} %get-tuple-element.20), channel_id=1, source_target_pairs={{0,1},{1,2},{2,3},{3,0},{4,5},{5,6},{6,7},{7,4},{8,9},{9,10},{10,1... | collective-permute-start | bytes 12296 | tf_op jit(solution)/shard_map/ppermute | solution.py:29
  7.9 43.9 %collective-permute-start.2 = (f32[2,8,4,128]{3,2,1,0:T(4,128)S(1)}, f32[2,8,4,128]{3,2,1,0:T(4,128)S(1)}, u32[]{:S(2)}, u32[]{:S(2)}) collective-permute-start(f32[2,8,4,128]{3,2,1,0:T(4,128)S(1)} %get-tuple-element.15), channel_id=1, source_target_pairs={{4,0},{0,4},{5,1},{1,5},{6,2},{2,6},{7,3},{3,7},{12,8},{8,12},{13,... | collective-permute-start | bytes 98312 | tf_op jit(solution)/shard_map/ppermute | solution.py:30
  14.8 0.7 %copy-start.3 = (s32[96,3]{0,1:T(4,128)S(1)}, s32[96,3]{0,1:T(4,128)}, u32[]{:S(2)}) copy-start(s32[96,3]{0,1:T(4,128)} %param.7) | copy-start | bytes 3460
  50.0 4.0 %collective-permute-start.3 = (f32[2,8,4,128]{3,2,1,0:T(4,128)S(1)}, f32[2,8,4,128]{3,2,1,0:T(4,128)S(1)}, u32[]{:S(2)}, u32[]{:S(2)}) collective-permute-start(f32[2,8,4,128]{3,2,1,0:T(4,128)S(1)} %get-tuple-element.16), channel_id=1, source_target_pairs={{0,4},{4,0},{1,5},{5,1},{2,6},{6,2},{3,7},{7,3},{8,12},{12,8},{9,1... | collective-permute-start | bytes 98312 | tf_op jit(solution)/shard_map/ppermute | solution.py:29
